TPU v7x, 8 devices: a whole 2x2x1 slice. The times are simulated.
8 devices in a mesh: dp: 1 (over z), col: 2 (over y), row: 4 (over x, core).
Axes of the slice: x: 2, y: 2, z: 1, core: 2. Of those that a mesh axis runs over, the one named last changes fastest.
Arguments:
- x_in: bfloat16 [2, 4096, 5120], P(None, ('dp', 'row'), 'col')
- ln_gamma: float32 [5120], P('col')
- w_in: bfloat16 [5120, 20480], P('row', 'col')
- w_out: bfloat16 [20480, 5120], P('row', 'col')
Outputs:
- output: bfloat16 [2, 4096, 5120], P(None, ('dp', 'row'), 'col')
All inputs are finite; a program needn't handle non-finite values.
Results may differ from a plain program's by a relative error of at most 0.00106.
Values are sent between devices in bfloat16 or wider.
A program may use at most 1 GiB of HBM per device.

v0:
```python
import jax
import jax.numpy as jnp
from jax import lax
from jax.sharding import PartitionSpec as P

LN_EPS = 1e-5


def solution(mesh):
    col_size = mesh.shape["col"]
    act_spec = P(None, ("dp", "row"), "col")

    def per_device(x_blk, gamma_blk, w_in_blk, w_out_blk):
        d_model = gamma_blk.shape[0] * col_size
        x_f32 = x_blk.astype(jnp.float32)
        row_stats = jnp.stack([jnp.sum(x_f32, axis=-1), jnp.sum(x_f32 * x_f32, axis=-1)])
        row_stats = lax.psum(row_stats, "col")
        row_mean = row_stats[0] / d_model
        row_var = row_stats[1] / d_model - row_mean * row_mean
        inv_std = lax.rsqrt(row_var + LN_EPS)
        z_norm = ((x_f32 - row_mean[..., None]) * inv_std[..., None] * gamma_blk).astype(jnp.bfloat16)
        z_panel = lax.all_gather(z_norm, "col", axis=2, tiled=True)
        w_in_panel = lax.all_gather(w_in_blk, "row", axis=0, tiled=True)
        hidden = jnp.dot(z_panel, w_in_panel, preferred_element_type=jnp.float32)
        hidden = jax.nn.gelu(hidden, approximate=True).astype(jnp.bfloat16)
        h_panel = lax.all_gather(hidden, "col", axis=2, tiled=True)
        w_out_panel = lax.all_gather(w_out_blk, "row", axis=0, tiled=True)
        branch = jnp.dot(h_panel, w_out_panel, preferred_element_type=jnp.float32)
        return (x_f32 + branch).astype(jnp.bfloat16)

    return jax.shard_map(per_device, mesh=mesh, in_specs=(act_spec, P("col"), P("row", "col"), P("row", "col")), out_specs=act_spec, check_vma=False)
```

profile of v0, /device:TPU:2, one launch (start us, length us, event | category | flops | bytes accessed | tf_op | source)
XLA Modules:
  0.0 2685.4 jit_solution(12621965436144822360)
XLA Ops:
  6.5 0.0 all-gather.5.cloned.1.call-start
  6.5 6.9 convert_reduce_fusion
  13.5 8.2 psum.7
  21.7 11.5 fusion.17
  33.2 0.0 all-gather.5.cloned.1.call-update
  33.3 0.0 all-gather.7.cloned.1.call-start
  33.3 0.7 all-gather.7.cloned.1.call-update
  34.0 0.0 all-gather.11.cloned.1.call-start
  34.1 0.7 all-gather.11.cloned.1.call-update
  34.8 0.2 all-gather.9.cloned.1.call-start
  35.0 243.4 %all-gather.5.cloned.1.call-done = bf16[2,1024,5120]{2,1,0:T(8,128)(2,1)} async-done(((bf16[2,1024,2560]{2,1,0:T(8,128)(2,1)}), bf16[2,1024,5120]{2,1,0:T(8,128)(2,1)}) %all-gather.5.cloned.1.call-update) | async-done | bytes 20971536 | tf_op jit(solution)/shard_map/all_gather | solution.py:22
  278.4 605.9 %all-gather.7.cloned.1.call-done = bf16[5120,10240]{1,0:T(8,128)(2,1)} async-done(((bf16[1280,10240]{1,0:T(8,128)(2,1)}), bf16[5120,10240]{1,0:T(8,128)(2,1)}) %all-gather.7.cloned.1.call-update) | async-done | bytes 104857616 | tf_op jit(solution)/shard_map/all_gather | solution.py:23
  884.3 241.3 %fusion.11 = bf16[2,1024,10240]{2,1,0:T(8,128)(2,1)} fusion(bf16[2,1024,5120]{2,1,0:T(8,128)(2,1)} %all-gather.5.cloned.1.call-done, bf16[5120,10240]{1,0:T(8,128)(2,1)} %all-gather.7.cloned.1.call-done), kind=kOutput, calls=%fused_computation.12 | convolution fusion | flops 214937108480 | bytes 167772160 | tf_op jit(solution)/shard_map/dot_general | solution.py:24
  1125.6 0.0 all-gather.9.cloned.1.call-update
  1125.6 365.7 %all-gather.11.cloned.1.call-done = bf16[20480,2560]{1,0:T(8,128)(2,1)} async-done(((bf16[5120,2560]{1,0:T(8,128)(2,1)}), bf16[20480,2560]{1,0:T(8,128)(2,1)}) %all-gather.11.cloned.1.call-update) | async-done | bytes 104857616 | tf_op jit(solution)/shard_map/all_gather | solution.py:27
  1491.4 956.2 %all-gather.9.cloned.1.call-done = bf16[2,1024,20480]{2,1,0:T(8,128)(2,1)} async-done(((bf16[2,1024,10240]{2,1,0:T(8,128)(2,1)}), bf16[2,1024,20480]{2,1,0:T(8,128)(2,1)}) %all-gather.9.cloned.1.call-update) | async-done | bytes 83886096 | tf_op jit(solution)/shard_map/all_gather | solution.py:26
  2447.6 231.4 %fusion.18 = bf16[2,1024,2560]{2,1,0:T(8,128)(2,1)} fusion(bf16[2,1024,2560]{2,1,0:T(8,128)(2,1)} %param.4, bf16[2,1024,20480]{2,1,0:T(8,128)(2,1)} %all-gather.9.cloned.1.call-done, bf16[20480,2560]{1,0:T(8,128)(2,1)} %all-gather.11.cloned.1.call-done), kind=kOutput, calls=%fused_computation.21 | convolution fusion | flops 214764093440 | bytes 209715200 | tf_op jit(solution)/shard_map/dot_general | solution.py:28
  (3 shorter events, 0.0 us)
Async XLA Ops:
  6.5 271.8 %all-gather.5.cloned.1.call-start = ((), (), s32[]{:S(2)}) async-start(), calls=%async_computation | async-start | bytes 31457280 | tf_op jit(solution)/shard_map/all_gather | solution.py:22
  33.3 851.0 %all-gather.7.cloned.1.call-start = ((), (), s32[]{:S(2)}) async-start(), calls=%async_computation.1 | async-start | bytes 131072000 | tf_op jit(solution)/shard_map/all_gather | solution.py:23
  34.0 1457.3 %all-gather.11.cloned.1.call-start = ((), (), s32[]{:S(2)}) async-start(), calls=%async_computation.3 | async-start | bytes 131072000 | tf_op jit(solution)/shard_map/all_gather | solution.py:27
  34.8 2412.8 %all-gather.9.cloned.1.call-start = ((), (), s32[]{:S(2)}) async-start(), calls=%async_computation.2 | async-start | bytes 125829120 | tf_op jit(solution)/shard_map/all_gather | solution.py:26
Sparse Core Ops, SparseCore 0:
  33.4 244.9 all-gather.4
  279.9 604.3 all-gather.6
  885.9 605.4 all-gather.10
  1492.7 954.7 all-gather.8
where the time goes:
time: 2690 us
  waiting for transfers between devices  2170 us (81%)
  matrix products  473 us (18%)
    all_gather x1, waiting for transfers between devices, per_device(): h_panel = lax.all_gather(hidden, 'col', axis=2, tiled=True)  956 us
    all_gather x1, waiting for transfers between devices, per_device(): w_in_panel = lax.all_gather(w_in_blk, 'row', axis=0, tiled=True)  606 us
    all_gather x1, waiting for transfers between devices, per_device(): w_out_panel = lax.all_gather(w_out_blk, 'row', axis=0, tiled=True)  366 us
    all_gather x1, waiting for transfers between devices, per_device(): z_panel = lax.all_gather(z_norm, 'col', axis=2, tiled=True)  243 us
    dot_general x1, matrix products, per_device(): hidden = jnp.dot(z_panel, w_in_panel, preferred_element_type=jnp.float32)  241 us
    dot_general x1, matrix products, per_device(): branch = jnp.dot(h_panel, w_out_panel, preferred_element_type=jnp.float32)  231 us
  transfers between devices with their start and end apart: 4, of which 4 were waited for; matrix products, arithmetic and copies ran while one was open for 9% of the time, Pallas kernels for 0%

commit v1 on v0

v1 whole, which is shorter than its diff:
```python
import functools
import math

import jax
import jax.numpy as jnp
from jax import lax
from jax.experimental import pallas as pl
from jax.experimental.pallas import tpu as pltpu
from jax.sharding import PartitionSpec as P

LN_EPS = 1e-5
MESH = pl.DeviceIdType.MESH
TN = 512
WINDOW = 8
EARLY = 8
TM = 256
GELU_C = math.sqrt(2 / math.pi)


def kernel(dims, x, g, w1, w2, y_out, xr, gr, w1_all, w2_all, hall,
           z, wt, hout, ln_a, ln_b, gv, acc, ht, w2t,
           xs, xrs, gs, xs1, xr1, ss1, sr1, fs1, fr1, xs2, xr2, ss2, sr2, fs2, fr2, hs, hr,
           lsem, csem, osem):
    n_mb, tok, dh, d4, hid, r4 = dims
    d_model = 2 * dh
    n1 = hid // TN
    n2 = r4 // TN
    col = lax.axis_index("col")
    row = lax.axis_index("row")
    far = 1 - col
    sib = row + 1 - 2 * lax.rem(row, 2)
    xn = lax.rem(row + 2, 4)
    xs_row = lax.rem(sib + 2, 4)
    to_col, to_x, to_sib = {"col": far}, {"row": xn}, {"row": sib}

    def remote(src, dst, ssem, rsem, dev):
        return pltpu.make_async_remote_copy(src_ref=src, dst_ref=dst, send_sem=ssem, recv_sem=rsem, device_id=dev, device_id_type=MESH)

    def cols(s):
        return pl.ds(pl.multiple_of(lax.rem(s, 2) * r4 + (s // 2) * TN, TN), TN)

    def rows2(c):
        return pl.ds(pl.multiple_of(c * TN, TN), TN)

    def x_move(m):
        return remote(x.at[m], xr.at[m], xs.at[m], xrs.at[m], to_col)

    def g_move():
        return remote(g, gr, gs.at[0], gs.at[1], to_col)

    def w1_x(s):
        return remote(w1.at[:, cols(s)], w1_all.at[row, :, cols(s)], xs1.at[s], xr1.at[s], to_x)

    def w1_sib(s):
        return remote(w1.at[:, cols(s)], w1_all.at[row, :, cols(s)], ss1.at[s], sr1.at[s], to_sib)

    def w1_fwd(s):
        return remote(w1_all.at[xn, :, cols(s)], w1_all.at[xn, :, cols(s)], fs1.at[s], fr1.at[s], to_sib)

    def w2_x(c):
        return remote(w2.at[rows2(c)], w2_all.at[row, rows2(c)], xs2.at[c], xr2.at[c], to_x)

    def w2_sib(c):
        return remote(w2.at[rows2(c)], w2_all.at[row, rows2(c)], ss2.at[c], sr2.at[c], to_sib)

    def w2_fwd(c):
        return remote(w2_all.at[xn, rows2(c)], w2_all.at[xn, rows2(c)], fs2.at[c], fr2.at[c], to_sib)

    def h_move(m, s):
        return remote(hall.at[col, m, :, cols(s)], hall.at[col, m, :, cols(s)], hs.at[m * n1 + s], hr.at[m * n1 + s], to_col)

    barrier = pltpu.get_barrier_semaphore()
    for dev in (to_col, to_x, to_sib):
        pl.semaphore_signal(barrier, inc=1, device_id=dev, device_id_type=MESH)
    pl.semaphore_wait(barrier, 3)

    g_move().start()
    for m in range(n_mb):
        x_move(m).start()

    def first_pieces(s, carry):
        w1_x(s).start()
        w1_sib(s).start()
        return carry

    lax.fori_loop(0, WINDOW, first_pieces, 0)

    def issue_after(s):
        @pl.when(s + WINDOW < n1)
        def _():
            w1_x(s + WINDOW).start()
            w1_sib(s + WINDOW).start()

        @pl.when(s + WINDOW >= n1)
        def _():
            w2_x(s + WINDOW - n1).start()
            w2_sib(s + WINDOW - n1).start()

    def layer_norm(m):
        x_move(m).wait_recv()

        def tile(t, carry):
            sl = pl.ds(pl.multiple_of(t * TM, TM), TM)
            near = pltpu.make_async_copy(x.at[m, sl], ln_a, lsem.at[0])
            other = pltpu.make_async_copy(xr.at[m, sl], ln_b, lsem.at[1])
            near.start()
            other.start()
            near.wait()
            other.wait()

            def strip(i, carry):
                rs = pl.ds(pl.multiple_of(i * 16, 16), 16)
                a = ln_a[rs, :].astype(jnp.float32)
                b = ln_b[rs, :].astype(jnp.float32)
                mean = (jnp.sum(a, axis=-1, keepdims=True) + jnp.sum(b, axis=-1, keepdims=True)) / d_model
                var = (jnp.sum(a * a, axis=-1, keepdims=True) + jnp.sum(b * b, axis=-1, keepdims=True)) / d_model - mean * mean
                inv = lax.rsqrt(var + LN_EPS)
                zr = pl.ds(pl.multiple_of(m * tok + t * TM + i * 16, 16), 16)
                z[zr, pl.ds(pl.multiple_of(col * dh, 128), dh)] = ((a - mean) * inv * gv[0:1, :]).astype(jnp.bfloat16)
                z[zr, pl.ds(pl.multiple_of(far * dh, 128), dh)] = ((b - mean) * inv * gv[1:2, :]).astype(jnp.bfloat16)
                return carry

            lax.fori_loop(0, TM // 16, strip, 0)
            return carry

        lax.fori_loop(0, tok // TM, tile, 0)

    def take_piece(s):
        w1_x(s).wait_recv()
        w1_fwd(s).start()
        issue_after(s)
        w1_sib(s).wait_recv()
        w1_fwd(s).wait_recv()

    def load_wt(s):
        copies = [pltpu.make_async_copy(w1.at[:, cols(s)], wt.at[pl.ds(pl.multiple_of(row * d4, d4), d4)], lsem.at[0])]
        for j, b in enumerate((sib, xn, xs_row)):
            copies.append(pltpu.make_async_copy(w1_all.at[b, :, cols(s)], wt.at[pl.ds(pl.multiple_of(b * d4, d4), d4)], lsem.at[j + 1]))
        for cp in copies:
            cp.start()
        for cp in copies:
            cp.wait()

    def first_product(m, s):
        def tile(t, carry):
            rs = pl.ds(pl.multiple_of(t * TM, TM), TM)
            zr = pl.ds(pl.multiple_of(m * tok + t * TM, TM), TM)
            u = jnp.dot(z[zr, :], wt[...], preferred_element_type=jnp.float32)
            h = 0.5 * u * (1.0 + jnp.tanh(GELU_C * (u + 0.044715 * (u * u * u))))
            hout[rs, :] = h.astype(jnp.bfloat16)
            return carry

        lax.fori_loop(0, tok // TM, tile, 0)
        cp = pltpu.make_async_copy(hout, hall.at[col, m, :, cols(s)], csem.at[0])
        cp.start()
        cp.wait()
        h_move(m, s).start()

    g_move().wait_recv()
    for i, src in enumerate((g, gr)):
        cp = pltpu.make_async_copy(src, gv.at[pl.ds(i, 1)], lsem.at[0])
        cp.start()
        cp.wait()
    layer_norm(0)

    def early_a(s, carry):
        take_piece(s)
        load_wt(s)
        first_product(0, s)
        return carry

    def early_b(s, carry):
        load_wt(s)
        first_product(1, s)
        return carry

    def rest(s, carry):
        take_piece(s)
        load_wt(s)

        def each(m, carry):
            first_product(m, s)
            return carry

        lax.fori_loop(0, n_mb, each, 0)
        return carry

    lax.fori_loop(0, EARLY, early_a, 0)
    layer_norm(1)
    lax.fori_loop(0, EARLY, early_b, 0)
    lax.fori_loop(EARLY, n1, rest, 0)

    def init(t, carry):
        m, q = t // (tok // TM), lax.rem(t, tok // TM)
        cp = pltpu.make_async_copy(x.at[m, pl.ds(pl.multiple_of(q * TM, TM), TM)], ln_a, lsem.at[0])
        cp.start()
        cp.wait()
        acc[pl.ds(pl.multiple_of(t * TM, TM), TM), :] = ln_a[...].astype(jnp.float32)
        return carry

    lax.fori_loop(0, n_mb * tok // TM, init, 0)

    def chunk(c, last):
        for m in range(n_mb):
            for k in range(2):
                h_move(m, 2 * c + k).wait_recv()
        w2_sib(c).wait_recv()
        blocks = (row, sib, xn, xs_row)

        def load(j):
            b, slot = blocks[j], j % 2
            hc = pl.ds(pl.multiple_of(lax.rem(b, 2) * r4 + c * TN, TN), TN)
            src = w2.at[rows2(c)] if j == 0 else w2_all.at[b, rows2(c)]
            return [pltpu.make_async_copy(src, w2t.at[slot], lsem.at[2 * slot])] + [
                pltpu.make_async_copy(hall.at[b // 2, m, :, hc], ht.at[slot, pl.ds(m * tok, tok)], csem.at[n_mb * slot + m]) for m in range(n_mb)]

        def start(j):
            for cp in load(j):
                cp.start()

        def wait(j):
            for cp in load(j):
                cp.wait()

        def product(j, drain):
            slot = j % 2

            def tile(t, carry):
                rs = pl.ds(pl.multiple_of(t * TM, TM), TM)

                def part(i, carry):
                    cs = pl.ds(pl.multiple_of(i * TN, TN), TN)
                    acc[rs, cs] += jnp.dot(ht[slot, rs, :], w2t[slot, :, cs], preferred_element_type=jnp.float32)
                    return carry

                lax.fori_loop(0, dh // TN, part, 0)
                if drain:
                    drain(t, rs)
                return carry

            lax.fori_loop(0, n_mb * tok // TM, tile, 0)

        start(0)
        start(1)
        wait(0)
        product(0, None)
        w2_x(c).wait_recv()
        w2_fwd(c).start()
        if not last:
            @pl.when(c + WINDOW < n2)
            def _():
                w2_x(c + WINDOW).start()
                w2_sib(c + WINDOW).start()
        start(2)
        wait(1)
        product(1, None)
        w2_fwd(c).wait_recv()
        start(3)
        wait(2)
        product(2, None)
        wait(3)
        if not last:
            product(3, None)
            return

        def out_copy(t, buf, sem):
            m, q = t // (tok // TM), lax.rem(t, tok // TM)
            return pltpu.make_async_copy(buf, y_out.at[m, pl.ds(pl.multiple_of(q * TM, TM), TM)], sem)

        def drain(t, rs):
            for p, buf in enumerate((ln_a, ln_b)):
                @pl.when(lax.rem(t, 2) == p)
                def _():
                    @pl.when(t >= 2)
                    def _():
                        out_copy(t - 2, buf, osem.at[p]).wait()
                    buf[...] = acc[rs, :].astype(jnp.bfloat16)
                    out_copy(t, buf, osem.at[p]).start()

        product(3, drain)
        steps = n_mb * tok // TM
        for p, buf in enumerate((ln_a, ln_b)):
            out_copy(steps - 2 + p, buf, osem.at[p]).wait()

    def middle(c, carry):
        chunk(c, False)
        return carry

    lax.fori_loop(0, n2 - 1, middle, 0)
    chunk(n2 - 1, True)

    g_move().wait_send()
    for m in range(n_mb):
        x_move(m).wait_send()

    def sent1(s, carry):
        w1_x(s).wait_send()
        w1_sib(s).wait_send()
        w1_fwd(s).wait_send()
        for m in range(n_mb):
            h_move(m, s).wait_send()
        return carry

    def sent2(c, carry):
        w2_x(c).wait_send()
        w2_sib(c).wait_send()
        w2_fwd(c).wait_send()
        return carry

    lax.fori_loop(0, n1, sent1, 0)
    lax.fori_loop(0, n2, sent2, 0)


def solution(mesh):
    act_spec = P(None, ("dp", "row"), "col")

    def per_device(x, gamma, w1, w2):
        n_mb, tok, dh = x.shape
        d4, hid = w1.shape
        r4 = w2.shape[0]
        n1, n2 = hid // TN, r4 // TN
        bf16, f32 = jnp.bfloat16, jnp.float32
        dma = pltpu.SemaphoreType.DMA
        any_spec = pl.BlockSpec(memory_space=pl.ANY)
        shapes = (
            jax.ShapeDtypeStruct((n_mb, tok, dh), bf16),
            jax.ShapeDtypeStruct((n_mb, tok, dh), bf16),
            jax.ShapeDtypeStruct((1, dh), f32),
            jax.ShapeDtypeStruct((4, d4, hid), bf16),
            jax.ShapeDtypeStruct((4, r4, dh), bf16),
            jax.ShapeDtypeStruct((2, n_mb, tok, hid), bf16),
        )
        outs = pl.pallas_call(
            functools.partial(kernel, (n_mb, tok, dh, d4, hid, r4)),
            out_shape=shapes,
            in_specs=[any_spec] * 4,
            out_specs=[any_spec] * len(shapes),
            scratch_shapes=[
                pltpu.VMEM((n_mb * tok, 2 * dh), bf16),
                pltpu.VMEM((4 * d4, TN), bf16),
                pltpu.VMEM((tok, TN), bf16),
                pltpu.VMEM((TM, dh), bf16),
                pltpu.VMEM((TM, dh), bf16),
                pltpu.VMEM((2, dh), f32),
                pltpu.VMEM((n_mb * tok, dh), f32),
                pltpu.VMEM((2, n_mb * tok, TN), bf16),
                pltpu.VMEM((2, TN, dh), bf16),
                dma((n_mb,)), dma((n_mb,)), dma((2,)),
                dma((n1,)), dma((n1,)), dma((n1,)), dma((n1,)), dma((n1,)), dma((n1,)),
                dma((n2,)), dma((n2,)), dma((n2,)), dma((n2,)), dma((n2,)), dma((n2,)),
                dma((n_mb * n1,)), dma((n_mb * n1,)),
                dma((4,)), dma((4,)), dma((2,)),
            ],
            compiler_params=pltpu.CompilerParams(collective_id=0, has_side_effects=True, vmem_limit_bytes=67043328),
        )(x, gamma.reshape(1, dh), w1, w2)
        return outs[0]

    return jax.shard_map(per_device, mesh=mesh, in_specs=(act_spec, P("col"), P("row", "col"), P("row", "col")), out_specs=act_spec, check_vma=False)
```

time: 2690 us -> 1200 us (0.45)
  waiting for transfers between devices: 2170 us -> 0 us
  Pallas kernels: 0 us -> 1180 us
  matrix products: 473 us -> 0 us
    all_gather x4 -> x0, waiting for transfers between devices: 2170 us -> none  [the longest x1 956 us: per_device(): h_panel = lax.all_gather(hidden, 'col', axis=2, tiled=True)]
    pallas_call x0 -> x1, Pallas kernels: none -> 1180 us  [per_device(): pl.pallas_call(functools.partial(kernel, (n_mb, tok, dh, d4, hid, r4)), o...]
    dot_general x2 -> x0, matrix products: 473 us -> none  [the longest x1 241 us: per_device(): hidden = jnp.dot(z_panel, w_in_panel, preferred_element_type=jnp.float32)]
  transfers between devices with their start and end apart: 4 -> 0, of which waited for: 4 -> 0; matrix products, arithmetic and copies ran while one was open for 9% -> 0% of each run, Pallas kernels for 0% -> 0%
where the time goes in v1:
time: 1200 us; the launch traced here: 1190 us
  Pallas kernels  1180 us (98%)
    pallas_call x1, Pallas kernels, per_device(): pl.pallas_call(functools.partial(kernel, (n_mb, tok, dh, d4, hid, r4)), o...  1180 us

profile of v1, /device:TPU:2, one launch (start us, length us, event | category | flops | bytes accessed | tf_op | source)
XLA Modules:
  0.0 1192.6 jit_solution(4057797935331538850)
XLA Ops:
  0.0 1.3 reshape.3.g
  1.3 1182.5 %shard_map.46 = (bf16[2,1024,2560]{2,1,0:T(8,128)(2,1)}, bf16[2,1024,2560]{2,1,0:T(8,128)(2,1)}, f32[1,2560]{1,0:T(1,128)}, bf16[4,1280,10240]{2,1,0:T(8,128)(2,...) custom-call(bf16[2,1024,2560]{2,1,0:T(8,128)(2,1)} %x.1, f32[1,2560]{1,0:T(1,128)} %reshape.3.g, ...), custom_call_target="tpu_custom_call" | custom-call | tf_op jit(solution)/shard_map/pallas_call | solution.py:333
  1183.9 8.7 copy.6

commit v2 on v1

v2 whole, which is shorter than its diff:
```python
import functools
import math

import jax
import jax.numpy as jnp
from jax import lax
from jax.experimental import pallas as pl
from jax.experimental.pallas import tpu as pltpu
from jax.sharding import PartitionSpec as P

LN_EPS = 1e-5
MESH = pl.DeviceIdType.MESH
TN = 512
WINDOW = 8
EARLY = 8
TM = 256
SUB = 256
GELU_C = math.sqrt(2 / math.pi)


def kernel(dims, x, g, w1, w2, y_out, xr, gr, w1_all, w2_all, hall,
           z, wt, hout, ln_a, ln_b, gv, acc,
           xs, xrs, gs, xs1, xr1, ss1, sr1, fs1, fr1, xs2, xr2, ss2, sr2, fs2, fr2, hs, hr,
           lsem, csem, osem, wsem):
    n_mb, tok, dh, d4, hid, r4 = dims
    d_model = 2 * dh
    n1 = hid // TN
    n2 = r4 // TN
    n_sub = TN // SUB
    col = lax.axis_index("col")
    row = lax.axis_index("row")
    far = 1 - col
    sib = row + 1 - 2 * lax.rem(row, 2)
    xn = lax.rem(row + 2, 4)
    xs_row = lax.rem(sib + 2, 4)
    to_col, to_x, to_sib = {"col": far}, {"row": xn}, {"row": sib}

    def remote(src, dst, ssem, rsem, dev):
        return pltpu.make_async_remote_copy(src_ref=src, dst_ref=dst, send_sem=ssem, recv_sem=rsem, device_id=dev, device_id_type=MESH)

    def cols(s):
        return pl.ds(pl.multiple_of(lax.rem(s, 2) * r4 + (s // 2) * TN, TN), TN)

    def rows2(p):
        if isinstance(p, int) and p >= n2 - 1:
            return pl.ds((n2 - 1) * TN + (p - n2 + 1) * SUB, SUB)
        return pl.ds(pl.multiple_of(p * TN, TN), TN)

    def x_move(m):
        return remote(x.at[m], xr.at[m], xs.at[m], xrs.at[m], to_col)

    def g_move():
        return remote(g, gr, gs.at[0], gs.at[1], to_col)

    def w1_x(s):
        return remote(w1.at[:, cols(s)], w1_all.at[row, s], xs1.at[s], xr1.at[s], to_x)

    def w1_sib(s):
        return remote(w1.at[:, cols(s)], w1_all.at[row, s], ss1.at[s], sr1.at[s], to_sib)

    def w1_fwd(s):
        return remote(w1_all.at[xn, s], w1_all.at[xn, s], fs1.at[s], fr1.at[s], to_sib)

    def w2_x(c):
        return remote(w2.at[rows2(c)], w2_all.at[row, rows2(c)], xs2.at[c], xr2.at[c], to_x)

    def w2_sib(c):
        return remote(w2.at[rows2(c)], w2_all.at[row, rows2(c)], ss2.at[c], sr2.at[c], to_sib)

    def w2_fwd(c):
        return remote(w2_all.at[xn, rows2(c)], w2_all.at[xn, rows2(c)], fs2.at[c], fr2.at[c], to_sib)

    def h_early(m, s):
        q = m * EARLY + s
        return remote(hall.at[col, s, m], hall.at[col, s, m], hs.at[q], hr.at[q], to_col)

    def h_pair(s):
        q = (n_mb - 1) * EARLY + s
        return remote(hall.at[col, s], hall.at[col, s], hs.at[q], hr.at[q], to_col)

    def h_last(k, u):
        s = n1 - 2 + k
        q = (n_mb - 1) * EARLY + n1 - 2 + k * n_sub + u
        return remote(hall.at[col, s, :, u], hall.at[col, s, :, u], hs.at[q], hr.at[q], to_col)

    barrier = pltpu.get_barrier_semaphore()
    for dev in (to_col, to_x, to_sib):
        pl.semaphore_signal(barrier, inc=1, device_id=dev, device_id_type=MESH)
    pl.semaphore_wait(barrier, 3)

    g_move().start()
    for m in range(n_mb):
        x_move(m).start()

    def first_pieces(s, carry):
        w1_x(s).start()
        w1_sib(s).start()
        return carry

    lax.fori_loop(0, WINDOW, first_pieces, 0)

    def issue_after(s):
        @pl.when(s + WINDOW < n1)
        def _():
            w1_x(s + WINDOW).start()
            w1_sib(s + WINDOW).start()

        @pl.when(s + WINDOW >= n1)
        def _():
            w2_x(s + WINDOW - n1).start()
            w2_sib(s + WINDOW - n1).start()

    def layer_norm(m):
        x_move(m).wait_recv()

        ga = gv[0:1, :]
        gb = gv[1:2, :]

        def tile(t, carry):
            sl = pl.ds(pl.multiple_of(t * TM, TM), TM)
            near = pltpu.make_async_copy(x.at[m, sl], ln_a, lsem.at[0])
            other = pltpu.make_async_copy(xr.at[m, sl], ln_b, lsem.at[1])
            near.start()
            other.start()
            near.wait()
            other.wait()

            def strip(i, carry):
                rs = pl.ds(pl.multiple_of(i * 16, 16), 16)
                a = ln_a[rs, :].astype(jnp.float32)
                b = ln_b[rs, :].astype(jnp.float32)
                mean = (jnp.sum(a, axis=-1, keepdims=True) + jnp.sum(b, axis=-1, keepdims=True)) / d_model
                var = (jnp.sum(a * a, axis=-1, keepdims=True) + jnp.sum(b * b, axis=-1, keepdims=True)) / d_model - mean * mean
                inv = lax.rsqrt(var + LN_EPS)
                zr = pl.ds(pl.multiple_of(m * tok + t * TM + i * 16, 16), 16)
                z[zr, pl.ds(pl.multiple_of(col * dh, 128), dh)] = ((a - mean) * inv * ga).astype(jnp.bfloat16)
                z[zr, pl.ds(pl.multiple_of(far * dh, 128), dh)] = ((b - mean) * inv * gb).astype(jnp.bfloat16)
                return carry

            lax.fori_loop(0, TM // 16, strip, 0)
            return carry

        lax.fori_loop(0, tok // TM, tile, 0)

    def take_piece(s):
        w1_x(s).wait_recv()
        w1_fwd(s).start()
        issue_after(s)
        w1_sib(s).wait_recv()
        w1_fwd(s).wait_recv()

    def wt_copies(s):
        base = lax.rem(s, 2) * (4 * d4)
        sem0 = 4 * lax.rem(s, 2)

        def rows(b):
            return wt.at[pl.ds(pl.multiple_of(base + b * d4, d4), d4)]

        copies = [pltpu.make_async_copy(w1.at[:, cols(s)], rows(row), lsem.at[sem0])]
        for j, b in enumerate((sib, xn, xs_row)):
            copies.append(pltpu.make_async_copy(w1_all.at[b, s], rows(b), lsem.at[sem0 + j + 1]))
        return copies

    def load_wt(s):
        for cp in wt_copies(s):
            cp.start()

    def wait_wt(s):
        for cp in wt_copies(s):
            cp.wait()

    def first_product(m, s):
        base = pl.multiple_of(lax.rem(s, 2) * (4 * d4), 4 * d4)

        def tile(t, carry):
            rs = pl.ds(pl.multiple_of(t * TM, TM), TM)
            zr = pl.ds(pl.multiple_of(m * tok + t * TM, TM), TM)
            u = jnp.dot(z[zr, :], wt[pl.ds(base, 4 * d4), :], preferred_element_type=jnp.float32)
            h = 0.5 * u * (1.0 + jnp.tanh(GELU_C * (u + 0.044715 * (u * u * u))))
            hout[rs, :] = h.astype(jnp.bfloat16)
            return carry

        lax.fori_loop(0, tok // TM, tile, 0)
        copies = [pltpu.make_async_copy(hout.at[:, u * SUB:(u + 1) * SUB], hall.at[col, s, m, u], csem.at[u]) for u in range(n_sub)]
        for cp in copies:
            cp.start()
        for cp in copies:
            cp.wait()

    g_move().wait_recv()
    for i, src in enumerate((g, gr)):
        cp = pltpu.make_async_copy(src, gv.at[pl.ds(i, 1)], lsem.at[0])
        cp.start()
        cp.wait()
    layer_norm(0)

    def early_a(s, carry):
        take_piece(s)
        load_wt(s)
        wait_wt(s)
        first_product(0, s)
        h_early(0, s).start()
        return carry

    def early_b(s, carry):
        wait_wt(s)

        @pl.when(s + 1 < EARLY)
        def _():
            load_wt(s + 1)

        first_product(1, s)
        h_early(1, s).start()
        return carry

    def both(s):
        take_piece(s)
        load_wt(s)
        wait_wt(s)

        def each(m, carry):
            first_product(m, s)
            return carry

        lax.fori_loop(0, n_mb, each, 0)

    def rest(s, carry):
        both(s)

        @pl.when(s < n1 - 2)
        def _():
            h_pair(s).start()

        return carry

    lax.fori_loop(0, EARLY, early_a, 0)
    layer_norm(1)
    load_wt(0)
    lax.fori_loop(0, EARLY, early_b, 0)
    lax.fori_loop(EARLY, n1, rest, 0)
    for u in range(n_sub):
        for k in range(2):
            h_last(k, u).start()

    def init(t, carry):
        m, q = t // (tok // TM), lax.rem(t, tok // TM)
        cp = pltpu.make_async_copy(x.at[m, pl.ds(pl.multiple_of(q * TM, TM), TM)], ln_a, lsem.at[0])
        cp.start()
        cp.wait()
        acc[pl.ds(pl.multiple_of(t * TM, TM), TM), :] = ln_a[...].astype(jnp.float32)
        return carry

    lax.fori_loop(0, n_mb * tok // TM, init, 0)

    def h_copies(c, u, g):
        size = TN if u is None else SUB
        subs = range(n_sub) if u is None else (u,)
        half = row // 2 if g == 0 else 1 - row // 2
        copies = []
        for k in range(2):
            for m in range(n_mb):
                for q, v in enumerate(subs):
                    dst = z.at[pl.ds(m * tok, tok), pl.ds(g * 2 * TN + k * size + q * SUB, SUB)]
                    copies.append(pltpu.make_async_copy(hall.at[half, 2 * c + k, m, v], dst, csem.at[len(copies) + 8 * g]))
        return copies

    def w2_copies(p, size, g, src_own, b, lane):
        k = lax.rem(b, 2)
        copies = []
        for i in range(dh // TN):
            rows = pl.ds(pl.multiple_of(g * (dh // TN) * 2 * TN + i * 2 * size + k * size, SUB), size)
            src = (w2.at[rows2(p)] if src_own else w2_all.at[b, rows2(p)]).at[:, i * TN:(i + 1) * TN]
            copies.append(pltpu.make_async_copy(src, wt.at[rows], wsem.at[lane * (dh // TN) + i]))
        return copies

    def product(size, g, drain):
        base = g * (dh // TN) * 2 * TN

        def tile(t, carry):
            rs = pl.ds(pl.multiple_of(t * TM, TM), TM)

            def part(i, carry):
                cs = pl.ds(pl.multiple_of(i * TN, TN), TN)
                ws = pl.ds(pl.multiple_of(base + i * 2 * size, SUB), 2 * size)
                acc[rs, cs] += jnp.dot(z[rs, g * 2 * TN:g * 2 * TN + 2 * size], wt[ws, :], preferred_element_type=jnp.float32)
                return carry

            lax.fori_loop(0, dh // TN, part, 0)
            if drain:
                drain(t, rs)
            return carry

        lax.fori_loop(0, n_mb * tok // TM, tile, 0)

    def out_copy(t, buf, sem):
        m, q = t // (tok // TM), lax.rem(t, tok // TM)
        return pltpu.make_async_copy(buf, y_out.at[m, pl.ds(pl.multiple_of(q * TM, TM), TM)], sem)

    def drain_tile(t, rs):
        for p, buf in enumerate((ln_a, ln_b)):
            @pl.when(lax.rem(t, 2) == p)
            def _():
                @pl.when(t >= 2)
                def _():
                    out_copy(t - 2, buf, osem.at[p]).wait()
                buf[...] = acc[rs, :].astype(jnp.bfloat16)
                out_copy(t, buf, osem.at[p]).start()

    def start(copies):
        for cp in copies:
            cp.start()

    def finish(copies):
        for cp in copies:
            cp.wait()

    def chunk(p, c, u, drain):
        size = TN if u is None else SUB
        own = w2_copies(p, size, 0, True, row, 0)
        start(own)

        def wait_h():
            if u is None:
                @pl.when(c < EARLY // 2)
                def _():
                    for m in range(n_mb):
                        for k in range(2):
                            h_early(m, 2 * c + k).wait_recv()

                @pl.when(c >= EARLY // 2)
                def _():
                    for k in range(2):
                        h_pair(2 * c + k).wait_recv()
            else:
                for k in range(2):
                    h_last(k, u).wait_recv()

        w2_sib(p).wait_recv()
        sib_w = w2_copies(p, size, 0, False, sib, 1)
        start(sib_w)

        @pl.when(row // 2 != col)
        def _():
            wait_h()

        h0 = h_copies(c, u, 0)
        h1 = h_copies(c, u, 1)
        start(h0)
        finish(own)
        finish(sib_w)
        finish(h0)
        product(size, 0, None)

        @pl.when(row // 2 == col)
        def _():
            wait_h()

        start(h1)
        w2_x(p).wait_recv()
        w2_fwd(p).start()
        if u is None:
            @pl.when(c + WINDOW < n2 - 1)
            def _():
                w2_x(c + WINDOW).start()
                w2_sib(c + WINDOW).start()
        x_w = w2_copies(p, size, 1, False, xn, 2)
        start(x_w)
        w2_fwd(p).wait_recv()
        f_w = w2_copies(p, size, 1, False, xs_row, 3)
        start(f_w)
        finish(h1)
        finish(x_w)
        finish(f_w)
        product(size, 1, drain)

    def middle(c, carry):
        chunk(c, c, None, None)

        @pl.when(c == 0)
        def _():
            for p in range(n2 - 1, n2 - 1 + n_sub):
                w2_x(p).start()
                w2_sib(p).start()

        return carry

    lax.fori_loop(0, n2 - 1, middle, 0)
    for u in range(n_sub):
        chunk(n2 - 1 + u, n2 - 1, u, drain_tile if u == n_sub - 1 else None)
    steps = n_mb * tok // TM
    for p, buf in enumerate((ln_a, ln_b)):
        out_copy(steps - 2 + p, buf, osem.at[p]).wait()

    g_move().wait_send()
    for m in range(n_mb):
        x_move(m).wait_send()

    def sent1(s, carry):
        w1_x(s).wait_send()
        w1_sib(s).wait_send()
        w1_fwd(s).wait_send()
        return carry

    def sent2(c, carry):
        w2_x(c).wait_send()
        w2_sib(c).wait_send()
        w2_fwd(c).wait_send()
        return carry

    def sent_early(s, carry):
        for m in range(n_mb):
            h_early(m, s).wait_send()
        return carry

    def sent_pair(s, carry):
        h_pair(s).wait_send()
        return carry

    lax.fori_loop(0, n1, sent1, 0)
    lax.fori_loop(0, n2 - 1, sent2, 0)
    for p in range(n2 - 1, n2 - 1 + n_sub):
        sent2(p, 0)
    lax.fori_loop(0, EARLY, sent_early, 0)
    lax.fori_loop(EARLY, n1 - 2, sent_pair, 0)
    for u in range(n_sub):
        for k in range(2):
            h_last(k, u).wait_send()


def solution(mesh):
    act_spec = P(None, ("dp", "row"), "col")

    def per_device(x, gamma, w1, w2):
        n_mb, tok, dh = x.shape
        d4, hid = w1.shape
        r4 = w2.shape[0]
        n1, n2 = hid // TN, r4 // TN
        n2p = n2 - 1 + TN // SUB
        nh = (n_mb - 1) * EARLY + n1 - 2 + 2 * (TN // SUB)
        bf16, f32 = jnp.bfloat16, jnp.float32
        dma = pltpu.SemaphoreType.DMA
        any_spec = pl.BlockSpec(memory_space=pl.ANY)
        shapes = (
            jax.ShapeDtypeStruct((n_mb, tok, dh), bf16),
            jax.ShapeDtypeStruct((n_mb, tok, dh), bf16),
            jax.ShapeDtypeStruct((1, dh), f32),
            jax.ShapeDtypeStruct((4, n1, d4, TN), bf16),
            jax.ShapeDtypeStruct((4, r4, dh), bf16),
            jax.ShapeDtypeStruct((2, n1, n_mb, TN // SUB, tok, SUB), bf16),
        )
        outs = pl.pallas_call(
            functools.partial(kernel, (n_mb, tok, dh, d4, hid, r4)),
            out_shape=shapes,
            in_specs=[any_spec] * 4,
            out_specs=[any_spec] * len(shapes),
            scratch_shapes=[
                pltpu.VMEM((n_mb * tok, 2 * dh), bf16),
                pltpu.VMEM((8 * d4, TN), bf16),
                pltpu.VMEM((tok, TN), bf16),
                pltpu.VMEM((TM, dh), bf16),
                pltpu.VMEM((TM, dh), bf16),
                pltpu.VMEM((2, dh), f32),
                pltpu.VMEM((n_mb * tok, dh), f32),
                dma((n_mb,)), dma((n_mb,)), dma((2,)),
                dma((n1,)), dma((n1,)), dma((n1,)), dma((n1,)), dma((n1,)), dma((n1,)),
                dma((n2p,)), dma((n2p,)), dma((n2p,)), dma((n2p,)), dma((n2p,)), dma((n2p,)),
                dma((nh,)), dma((nh,)),
                dma((8,)), dma((16,)), dma((2,)), dma((4 * (dh // TN),)),
            ],
            compiler_params=pltpu.CompilerParams(collective_id=0, has_side_effects=True, vmem_limit_bytes=67043328),
        )(x, gamma.reshape(1, dh), w1, w2)
        return outs[0]

    return jax.shard_map(per_device, mesh=mesh, in_specs=(act_spec, P("col"), P("row", "col"), P("row", "col")), out_specs=act_spec, check_vma=False)
```

time: 1200 us -> 1170 us (0.975)
  Pallas kernels: 1180 us -> 1160 us
    pallas_call x1, Pallas kernels: 1180 us -> 1160 us  [per_device(): pl.pallas_call(functools.partial(kernel, (n_mb, tok, dh, d4, hid, r4)), o...]
where the time goes in v2:
time: 1170 us
  Pallas kernels  1160 us (99%)
    pallas_call x1, Pallas kernels, per_device(): pl.pallas_call(functools.partial(kernel, (n_mb, tok, dh, d4, hid, r4)), o...  1160 us

profile of v2, /device:TPU:2, one launch (start us, length us, event | category | flops | bytes accessed | tf_op | source)
XLA Modules:
  0.0 1170.9 jit_solution(6443909576774961826)
XLA Ops:
  0.0 1.3 reshape.3.g
  1.3 1160.9 %shard_map.46 = (bf16[2,1024,2560]{2,1,0:T(8,128)(2,1)}, bf16[2,1024,2560]{2,1,0:T(8,128)(2,1)}, f32[1,2560]{1,0:T(1,128)}, bf16[4,20,1280,512]{3,2,1,0:T(8,128)...) custom-call(bf16[2,1024,2560]{2,1,0:T(8,128)(2,1)} %x.1, f32[1,2560]{1,0:T(1,128)} %reshape.3.g, ...), custom_call_target="tpu_custom_call" | custom-call | tf_op jit(solution)/shard_map/pallas_call | solution.py:451
  1162.2 8.7 copy.6

commit v3 on v2

--- a/solution.py
+++ b/solution.py
@@ -14,12 +14,13 @@
 WINDOW = 8
 EARLY = 8
 TM = 256
-SUB = 256
+SUB = 128
+LAST = (256, 128, 128)
 GELU_C = math.sqrt(2 / math.pi)
 
 
 def kernel(dims, x, g, w1, w2, y_out, xr, gr, w1_all, w2_all, hall,
-           z, wt, hout, ln_a, ln_b, gv, acc,
+           z, wt, hout, ln_a, ln_b, g_rows, gv, acc,
            xs, xrs, gs, xs1, xr1, ss1, sr1, fs1, fr1, xs2, xr2, ss2, sr2, fs2, fr2, hs, hr,
            lsem, csem, osem, wsem):
     n_mb, tok, dh, d4, hid, r4 = dims
@@ -27,12 +28,14 @@
     n1 = hid // TN
     n2 = r4 // TN
     n_sub = TN // SUB
+    last_at = [sum(LAST[:u]) for u in range(len(LAST))]
     col = lax.axis_index("col")
     row = lax.axis_index("row")
     far = 1 - col
     sib = row + 1 - 2 * lax.rem(row, 2)
     xn = lax.rem(row + 2, 4)
     xs_row = lax.rem(sib + 2, 4)
+    diagonal = row // 2 == col
     to_col, to_x, to_sib = {"col": far}, {"row": xn}, {"row": sib}
 
     def remote(src, dst, ssem, rsem, dev):
@@ -43,7 +46,7 @@
 
     def rows2(p):
         if isinstance(p, int) and p >= n2 - 1:
-            return pl.ds((n2 - 1) * TN + (p - n2 + 1) * SUB, SUB)
+            return pl.ds((n2 - 1) * TN + last_at[p - n2 + 1], LAST[p - n2 + 1])
         return pl.ds(pl.multiple_of(p * TN, TN), TN)
 
     def x_move(m):
@@ -80,8 +83,9 @@
 
     def h_last(k, u):
         s = n1 - 2 + k
-        q = (n_mb - 1) * EARLY + n1 - 2 + k * n_sub + u
-        return remote(hall.at[col, s, :, u], hall.at[col, s, :, u], hs.at[q], hr.at[q], to_col)
+        q = (n_mb - 1) * EARLY + n1 - 2 + k * len(LAST) + u
+        subs = pl.ds(last_at[u] // SUB, LAST[u] // SUB)
+        return remote(hall.at[col, s, :, subs], hall.at[col, s, :, subs], hs.at[q], hr.at[q], to_col)
 
     barrier = pltpu.get_barrier_semaphore()
     for dev in (to_col, to_x, to_sib):
@@ -189,9 +193,11 @@
 
     g_move().wait_recv()
     for i, src in enumerate((g, gr)):
-        cp = pltpu.make_async_copy(src, gv.at[pl.ds(i, 1)], lsem.at[0])
+        cp = pltpu.make_async_copy(src, g_rows.at[i], lsem.at[0])
         cp.start()
         cp.wait()
+        for j in range(dh // 128):
+            gv[i:i + 1, j * 128:(j + 1) * 128] = g_rows[i, j:j + 1, :]
     layer_norm(0)
 
     def early_a(s, carry):
@@ -238,7 +244,7 @@
     load_wt(0)
     lax.fori_loop(0, EARLY, early_b, 0)
     lax.fori_loop(EARLY, n1, rest, 0)
-    for u in range(n_sub):
+    for u in range(len(LAST)):
         for k in range(2):
             h_last(k, u).start()
 
@@ -253,15 +259,15 @@
     lax.fori_loop(0, n_mb * tok // TM, init, 0)
 
     def h_copies(c, u, g):
-        size = TN if u is None else SUB
-        subs = range(n_sub) if u is None else (u,)
+        size = TN if u is None else LAST[u]
+        subs = range(n_sub) if u is None else range(last_at[u] // SUB, (last_at[u] + LAST[u]) // SUB)
         half = row // 2 if g == 0 else 1 - row // 2
         copies = []
         for k in range(2):
             for m in range(n_mb):
                 for q, v in enumerate(subs):
                     dst = z.at[pl.ds(m * tok, tok), pl.ds(g * 2 * TN + k * size + q * SUB, SUB)]
-                    copies.append(pltpu.make_async_copy(hall.at[half, 2 * c + k, m, v], dst, csem.at[len(copies) + 8 * g]))
+                    copies.append(pltpu.make_async_copy(hall.at[half, 2 * c + k, m, v], dst, csem.at[len(copies) + 4 * n_sub * g]))
         return copies
 
     def w2_copies(p, size, g, src_own, b, lane):
@@ -273,19 +279,16 @@
             copies.append(pltpu.make_async_copy(src, wt.at[rows], wsem.at[lane * (dh // TN) + i]))
         return copies
 
-    def product(size, g, drain):
+    def product(size, g, drain=None):
         base = g * (dh // TN) * 2 * TN
 
         def tile(t, carry):
             rs = pl.ds(pl.multiple_of(t * TM, TM), TM)
 
-            def part(i, carry):
-                cs = pl.ds(pl.multiple_of(i * TN, TN), TN)
-                ws = pl.ds(pl.multiple_of(base + i * 2 * size, SUB), 2 * size)
+            for i in range(dh // TN):
+                cs = slice(i * TN, (i + 1) * TN)
+                ws = slice(base + i * 2 * size, base + (i + 1) * 2 * size)
                 acc[rs, cs] += jnp.dot(z[rs, g * 2 * TN:g * 2 * TN + 2 * size], wt[ws, :], preferred_element_type=jnp.float32)
-                return carry
-
-            lax.fori_loop(0, dh // TN, part, 0)
             if drain:
                 drain(t, rs)
             return carry
@@ -314,8 +317,8 @@
         for cp in copies:
             cp.wait()
 
-    def chunk(p, c, u, drain):
-        size = TN if u is None else SUB
+    def chunk(p, c, u, drain=None):
+        size = TN if u is None else LAST[u]
         own = w2_copies(p, size, 0, True, row, 0)
         start(own)
 
@@ -338,24 +341,26 @@
         w2_sib(p).wait_recv()
         sib_w = w2_copies(p, size, 0, False, sib, 1)
         start(sib_w)
-
-        @pl.when(row // 2 != col)
-        def _():
-            wait_h()
-
         h0 = h_copies(c, u, 0)
         h1 = h_copies(c, u, 1)
-        start(h0)
-        finish(own)
-        finish(sib_w)
-        finish(h0)
-        product(size, 0, None)
-
-        @pl.when(row // 2 == col)
-        def _():
-            wait_h()
-
-        start(h1)
+        x_w = w2_copies(p, size, 1, False, xn, 2)
+        f_w = w2_copies(p, size, 1, False, xs_row, 3)
+
+        def near_half():
+            finish(own)
+            finish(sib_w)
+            finish(h0)
+            product(size, 0)
+
+        @pl.when(diagonal)
+        def _():
+            start(h0)
+            near_half()
+
+        @pl.when(jnp.logical_not(diagonal))
+        def _():
+            start(h1)
+
         w2_x(p).wait_recv()
         w2_fwd(p).start()
         if u is None:
@@ -363,10 +368,19 @@
             def _():
                 w2_x(c + WINDOW).start()
                 w2_sib(c + WINDOW).start()
-        x_w = w2_copies(p, size, 1, False, xn, 2)
         start(x_w)
+        wait_h()
+
+        @pl.when(diagonal)
+        def _():
+            start(h1)
+
+        @pl.when(jnp.logical_not(diagonal))
+        def _():
+            start(h0)
+            near_half()
+
         w2_fwd(p).wait_recv()
-        f_w = w2_copies(p, size, 1, False, xs_row, 3)
         start(f_w)
         finish(h1)
         finish(x_w)
@@ -374,19 +388,19 @@
         product(size, 1, drain)
 
     def middle(c, carry):
-        chunk(c, c, None, None)
+        chunk(c, c, None)
 
         @pl.when(c == 0)
         def _():
-            for p in range(n2 - 1, n2 - 1 + n_sub):
+            for p in range(n2 - 1, n2 - 1 + len(LAST)):
                 w2_x(p).start()
                 w2_sib(p).start()
 
         return carry
 
     lax.fori_loop(0, n2 - 1, middle, 0)
-    for u in range(n_sub):
-        chunk(n2 - 1 + u, n2 - 1, u, drain_tile if u == n_sub - 1 else None)
+    for u in range(len(LAST)):
+        chunk(n2 - 1 + u, n2 - 1, u, drain_tile if u == len(LAST) - 1 else None)
     steps = n_mb * tok // TM
     for p, buf in enumerate((ln_a, ln_b)):
         out_copy(steps - 2 + p, buf, osem.at[p]).wait()
@@ -418,11 +432,11 @@
 
     lax.fori_loop(0, n1, sent1, 0)
     lax.fori_loop(0, n2 - 1, sent2, 0)
-    for p in range(n2 - 1, n2 - 1 + n_sub):
+    for p in range(n2 - 1, n2 - 1 + len(LAST)):
         sent2(p, 0)
     lax.fori_loop(0, EARLY, sent_early, 0)
     lax.fori_loop(EARLY, n1 - 2, sent_pair, 0)
-    for u in range(n_sub):
+    for u in range(len(LAST)):
         for k in range(2):
             h_last(k, u).wait_send()
 
@@ -435,15 +449,15 @@
         d4, hid = w1.shape
         r4 = w2.shape[0]
         n1, n2 = hid // TN, r4 // TN
-        n2p = n2 - 1 + TN // SUB
-        nh = (n_mb - 1) * EARLY + n1 - 2 + 2 * (TN // SUB)
+        n2p = n2 - 1 + len(LAST)
+        nh = (n_mb - 1) * EARLY + n1 - 2 + 2 * len(LAST)
         bf16, f32 = jnp.bfloat16, jnp.float32
         dma = pltpu.SemaphoreType.DMA
         any_spec = pl.BlockSpec(memory_space=pl.ANY)
         shapes = (
             jax.ShapeDtypeStruct((n_mb, tok, dh), bf16),
             jax.ShapeDtypeStruct((n_mb, tok, dh), bf16),
-            jax.ShapeDtypeStruct((1, dh), f32),
+            jax.ShapeDtypeStruct((dh // 128, 128), f32),
             jax.ShapeDtypeStruct((4, n1, d4, TN), bf16),
             jax.ShapeDtypeStruct((4, r4, dh), bf16),
             jax.ShapeDtypeStruct((2, n1, n_mb, TN // SUB, tok, SUB), bf16),
@@ -459,16 +473,17 @@
                 pltpu.VMEM((tok, TN), bf16),
                 pltpu.VMEM((TM, dh), bf16),
                 pltpu.VMEM((TM, dh), bf16),
+                pltpu.VMEM((2, dh // 128, 128), f32),
                 pltpu.VMEM((2, dh), f32),
                 pltpu.VMEM((n_mb * tok, dh), f32),
                 dma((n_mb,)), dma((n_mb,)), dma((2,)),
                 dma((n1,)), dma((n1,)), dma((n1,)), dma((n1,)), dma((n1,)), dma((n1,)),
                 dma((n2p,)), dma((n2p,)), dma((n2p,)), dma((n2p,)), dma((n2p,)), dma((n2p,)),
                 dma((nh,)), dma((nh,)),
-                dma((8,)), dma((16,)), dma((2,)), dma((4 * (dh // TN),)),
+                dma((8,)), dma((8 * (TN // SUB),)), dma((2,)), dma((4 * (dh // TN),)),
             ],
             compiler_params=pltpu.CompilerParams(collective_id=0, has_side_effects=True, vmem_limit_bytes=67043328),
-        )(x, gamma.reshape(1, dh), w1, w2)
+        )(x, gamma.reshape(dh // 128, 128), w1, w2)
         return outs[0]
 
     return jax.shard_map(per_device, mesh=mesh, in_specs=(act_spec, P("col"), P("row", "col"), P("row", "col")), out_specs=act_spec, check_vma=False)

time: 1170 us -> 1160 us (level)
  no operation moved by 1% of the time
where the time goes in v3:
time: 1160 us
  Pallas kernels  1150 us (99%)
    pallas_call x1, Pallas kernels, per_device(): pl.pallas_call(functools.partial(kernel, (n_mb, tok, dh, d4, hid, r4)), o...  1150 us

profile of v3, /device:TPU:2, one launch (start us, length us, event | category | flops | bytes accessed | tf_op | source)
XLA Modules:
  0.0 1158.3 jit_solution(18062345293452713707)
XLA Ops:
  0.0 1149.5 %shard_map.46 = (bf16[2,1024,2560]{2,1,0:T(8,128)(2,1)}, bf16[2,1024,2560]{2,1,0:T(8,128)(2,1)}, f32[20,128]{1,0:T(8,128)}, bf16[4,20,1280,512]{3,2,1,0:T(8,128)...) custom-call(bf16[2,1024,2560]{2,1,0:T(8,128)(2,1)} %x.1, f32[20,128]{1,0:T(8,128)} %bitcast.1, ...), custom_call_target="tpu_custom_call" | custom-call | tf_op jit(solution)/shard_map/pallas_call | solution.py:465
  1149.5 8.7 copy.6

commit v4 on v3

--- a/solution.py
+++ b/solution.py
@@ -16,6 +16,7 @@
 TM = 256
 SUB = 128
 LAST = (256, 128, 128)
+TAIL = ((2, 0, 256), (2, 256, 256), (1, 0, 256), (1, 256, 128), (1, 384, 128))
 GELU_C = math.sqrt(2 / math.pi)
 
 
@@ -29,6 +30,7 @@
     n2 = r4 // TN
     n_sub = TN // SUB
     last_at = [sum(LAST[:u]) for u in range(len(LAST))]
+    full = n2 - TAIL[0][0]
     col = lax.axis_index("col")
     row = lax.axis_index("row")
     far = 1 - col
@@ -45,8 +47,9 @@
         return pl.ds(pl.multiple_of(lax.rem(s, 2) * r4 + (s // 2) * TN, TN), TN)
 
     def rows2(p):
-        if isinstance(p, int) and p >= n2 - 1:
-            return pl.ds((n2 - 1) * TN + last_at[p - n2 + 1], LAST[p - n2 + 1])
+        if isinstance(p, int) and p >= full:
+            back, at, size = TAIL[p - full]
+            return pl.ds((n2 - back) * TN + at, size)
         return pl.ds(pl.multiple_of(p * TN, TN), TN)
 
     def x_move(m):
@@ -258,9 +261,9 @@
 
     lax.fori_loop(0, n_mb * tok // TM, init, 0)
 
-    def h_copies(c, u, g):
-        size = TN if u is None else LAST[u]
-        subs = range(n_sub) if u is None else range(last_at[u] // SUB, (last_at[u] + LAST[u]) // SUB)
+    def h_copies(c, piece, g):
+        at, size = piece
+        subs = range(at // SUB, (at + size) // SUB)
         half = row // 2 if g == 0 else 1 - row // 2
         copies = []
         for k in range(2):
@@ -317,13 +320,13 @@
         for cp in copies:
             cp.wait()
 
-    def chunk(p, c, u, drain=None):
-        size = TN if u is None else LAST[u]
+    def chunk(p, c, piece, drain=None):
+        size = piece[1]
         own = w2_copies(p, size, 0, True, row, 0)
         start(own)
 
         def wait_h():
-            if u is None:
+            if not isinstance(c, int):
                 @pl.when(c < EARLY // 2)
                 def _():
                     for m in range(n_mb):
@@ -334,15 +337,18 @@
                 def _():
                     for k in range(2):
                         h_pair(2 * c + k).wait_recv()
-            else:
+            elif c == n2 - 1:
                 for k in range(2):
-                    h_last(k, u).wait_recv()
+                    h_last(k, last_at.index(piece[0])).wait_recv()
+            elif piece[0] == 0:
+                for k in range(2):
+                    h_pair(2 * c + k).wait_recv()
 
         w2_sib(p).wait_recv()
         sib_w = w2_copies(p, size, 0, False, sib, 1)
         start(sib_w)
-        h0 = h_copies(c, u, 0)
-        h1 = h_copies(c, u, 1)
+        h0 = h_copies(c, piece, 0)
+        h1 = h_copies(c, piece, 1)
         x_w = w2_copies(p, size, 1, False, xn, 2)
         f_w = w2_copies(p, size, 1, False, xs_row, 3)
 
@@ -363,11 +369,6 @@
 
         w2_x(p).wait_recv()
         w2_fwd(p).start()
-        if u is None:
-            @pl.when(c + WINDOW < n2 - 1)
-            def _():
-                w2_x(c + WINDOW).start()
-                w2_sib(c + WINDOW).start()
         start(x_w)
         wait_h()
 
@@ -388,19 +389,19 @@
         product(size, 1, drain)
 
     def middle(c, carry):
-        chunk(c, c, None)
+        chunk(c, c, (0, TN))
 
         @pl.when(c == 0)
         def _():
-            for p in range(n2 - 1, n2 - 1 + len(LAST)):
+            for p in range(full, full + len(TAIL)):
                 w2_x(p).start()
                 w2_sib(p).start()
 
         return carry
 
-    lax.fori_loop(0, n2 - 1, middle, 0)
-    for u in range(len(LAST)):
-        chunk(n2 - 1 + u, n2 - 1, u, drain_tile if u == len(LAST) - 1 else None)
+    lax.fori_loop(0, full, middle, 0)
+    for i, (back, at, size) in enumerate(TAIL):
+        chunk(full + i, n2 - back, (at, size), drain_tile if i == len(TAIL) - 1 else None)
     steps = n_mb * tok // TM
     for p, buf in enumerate((ln_a, ln_b)):
         out_copy(steps - 2 + p, buf, osem.at[p]).wait()
@@ -431,8 +432,8 @@
         return carry
 
     lax.fori_loop(0, n1, sent1, 0)
-    lax.fori_loop(0, n2 - 1, sent2, 0)
-    for p in range(n2 - 1, n2 - 1 + len(LAST)):
+    lax.fori_loop(0, full, sent2, 0)
+    for p in range(full, full + len(TAIL)):
         sent2(p, 0)
     lax.fori_loop(0, EARLY, sent_early, 0)
     lax.fori_loop(EARLY, n1 - 2, sent_pair, 0)
@@ -449,7 +450,7 @@
         d4, hid = w1.shape
         r4 = w2.shape[0]
         n1, n2 = hid // TN, r4 // TN
-        n2p = n2 - 1 + len(LAST)
+        n2p = n2 - TAIL[0][0] + len(TAIL)
         nh = (n_mb - 1) * EARLY + n1 - 2 + 2 * len(LAST)
         bf16, f32 = jnp.bfloat16, jnp.float32
         dma = pltpu.SemaphoreType.DMA

time: 1160 us -> 1160 us (level)
  no operation moved by 1% of the time
where the time goes in v4:
time: 1160 us; the launch traced here: 1150 us
  Pallas kernels  1150 us (99%)
    pallas_call x1, Pallas kernels, per_device(): pl.pallas_call(functools.partial(kernel, (n_mb, tok, dh, d4, hid, r4)), o...  1150 us

profile of v4, /device:TPU:2, one launch (start us, length us, event | category | flops | bytes accessed | tf_op | source)
XLA Modules:
  0.0 1154.7 jit_solution(4985665107850891118)
XLA Ops:
  0.0 1146.0 %shard_map.46 = (bf16[2,1024,2560]{2,1,0:T(8,128)(2,1)}, bf16[2,1024,2560]{2,1,0:T(8,128)(2,1)}, f32[20,128]{1,0:T(8,128)}, bf16[4,20,1280,512]{3,2,1,0:T(8,128)...) custom-call(bf16[2,1024,2560]{2,1,0:T(8,128)(2,1)} %x.1, f32[20,128]{1,0:T(8,128)} %bitcast.1, ...), custom_call_target="tpu_custom_call" | custom-call | tf_op jit(solution)/shard_map/pallas_call | solution.py:466
  1146.0 8.7 copy.6

commit v5 on v4

--- a/solution.py
+++ b/solution.py
@@ -90,6 +90,26 @@
         subs = pl.ds(last_at[u] // SUB, LAST[u] // SUB)
         return remote(hall.at[col, s, :, subs], hall.at[col, s, :, subs], hs.at[q], hr.at[q], to_col)
 
+    def h_end(k, m):
+        q = (n_mb - 1) * EARLY + n1 - 2 + 2 * len(LAST) + k * n_mb + m
+        u = len(LAST) - 1
+        ref = hall.at[col, n1 - 2 + k, m, pl.ds(last_at[u] // SUB, LAST[u] // SUB)]
+        return remote(ref, ref, hs.at[q], hr.at[q], to_col)
+
+    p_end = full + len(TAIL) - 1
+    split = (dh // TN + 1) // 2
+    end_parts = (range(split), range(split, dh // TN))
+
+    def end_ref(ref, part):
+        i = end_parts[part]
+        return ref.at[rows2(p_end), i[0] * TN:(i[-1] + 1) * TN]
+
+    def w2_x_end(part):
+        return remote(end_ref(w2, part), end_ref(w2_all.at[row], part), xs2.at[p_end + part], xr2.at[p_end + part], to_x)
+
+    def w2_fwd_end(part):
+        return remote(end_ref(w2_all.at[xn], part), end_ref(w2_all.at[xn], part), fs2.at[p_end + part], fr2.at[p_end + part], to_sib)
+
     barrier = pltpu.get_barrier_semaphore()
     for dev in (to_col, to_x, to_sib):
         pl.semaphore_signal(barrier, inc=1, device_id=dev, device_id_type=MESH)
@@ -247,9 +267,12 @@
     load_wt(0)
     lax.fori_loop(0, EARLY, early_b, 0)
     lax.fori_loop(EARLY, n1, rest, 0)
-    for u in range(len(LAST)):
+    for u in range(len(LAST) - 1):
         for k in range(2):
             h_last(k, u).start()
+    for m in range(n_mb):
+        for k in range(2):
+            h_end(k, m).start()
 
     def init(t, carry):
         m, q = t // (tok // TM), lax.rem(t, tok // TM)
@@ -261,34 +284,34 @@
 
     lax.fori_loop(0, n_mb * tok // TM, init, 0)
 
-    def h_copies(c, piece, g):
+    def h_copies(c, piece, g, mbs=None):
         at, size = piece
         subs = range(at // SUB, (at + size) // SUB)
         half = row // 2 if g == 0 else 1 - row // 2
         copies = []
         for k in range(2):
-            for m in range(n_mb):
+            for m in mbs or range(n_mb):
                 for q, v in enumerate(subs):
                     dst = z.at[pl.ds(m * tok, tok), pl.ds(g * 2 * TN + k * size + q * SUB, SUB)]
-                    copies.append(pltpu.make_async_copy(hall.at[half, 2 * c + k, m, v], dst, csem.at[len(copies) + 4 * n_sub * g]))
+                    copies.append(pltpu.make_async_copy(hall.at[half, 2 * c + k, m, v], dst, csem.at[((g * 2 + k) * n_mb + m) * n_sub + q]))
         return copies
 
-    def w2_copies(p, size, g, src_own, b, lane):
+    def w2_copies(p, size, g, src_own, b, lane, parts=None):
         k = lax.rem(b, 2)
         copies = []
-        for i in range(dh // TN):
+        for i in parts or range(dh // TN):
             rows = pl.ds(pl.multiple_of(g * (dh // TN) * 2 * TN + i * 2 * size + k * size, SUB), size)
             src = (w2.at[rows2(p)] if src_own else w2_all.at[b, rows2(p)]).at[:, i * TN:(i + 1) * TN]
             copies.append(pltpu.make_async_copy(src, wt.at[rows], wsem.at[lane * (dh // TN) + i]))
         return copies
 
-    def product(size, g, drain=None):
+    def product(size, g, drain=None, mbs=None, parts=None):
         base = g * (dh // TN) * 2 * TN
 
         def tile(t, carry):
             rs = pl.ds(pl.multiple_of(t * TM, TM), TM)
 
-            for i in range(dh // TN):
+            for i in parts or range(dh // TN):
                 cs = slice(i * TN, (i + 1) * TN)
                 ws = slice(base + i * 2 * size, base + (i + 1) * 2 * size)
                 acc[rs, cs] += jnp.dot(z[rs, g * 2 * TN:g * 2 * TN + 2 * size], wt[ws, :], preferred_element_type=jnp.float32)
@@ -296,7 +319,8 @@
                 drain(t, rs)
             return carry
 
-        lax.fori_loop(0, n_mb * tok // TM, tile, 0)
+        mbs = mbs or range(n_mb)
+        lax.fori_loop(mbs[0] * tok // TM, (mbs[-1] + 1) * tok // TM, tile, 0)
 
     def out_copy(t, buf, sem):
         m, q = t // (tok // TM), lax.rem(t, tok // TM)
@@ -393,15 +417,103 @@
 
         @pl.when(c == 0)
         def _():
-            for p in range(full, full + len(TAIL)):
+            for p in range(full, p_end):
                 w2_x(p).start()
                 w2_sib(p).start()
+            for part in range(2):
+                w2_x_end(part).start()
+            w2_sib(p_end).start()
 
         return carry
 
     lax.fori_loop(0, full, middle, 0)
-    for i, (back, at, size) in enumerate(TAIL):
-        chunk(full + i, n2 - back, (at, size), drain_tile if i == len(TAIL) - 1 else None)
+    for i, (back, at, size) in enumerate(TAIL[:-1]):
+        chunk(full + i, n2 - back, (at, size))
+
+    def end_chunk():
+        c, piece, size = n2 - 1, TAIL[-1][1:], TAIL[-1][2]
+        own = w2_copies(p_end, size, 0, True, row, 0)
+        start(own)
+        w2_sib(p_end).wait_recv()
+        sib_w = w2_copies(p_end, size, 0, False, sib, 1)
+        start(sib_w)
+        h0 = [h_copies(c, piece, 0, (m,)) for m in range(n_mb)]
+        h1 = [h_copies(c, piece, 1, (m,)) for m in range(n_mb)]
+        x_w = [w2_copies(p_end, size, 1, False, xn, 2, i) for i in end_parts]
+        f_w = [w2_copies(p_end, size, 1, False, xs_row, 3, i) for i in end_parts]
+
+        def wait_h(m):
+            for k in range(2):
+                h_end(k, m).wait_recv()
+
+        @pl.when(diagonal)
+        def _():
+            for m in range(n_mb):
+                start(h0[m])
+            finish(own)
+            finish(sib_w)
+            for m in range(n_mb):
+                finish(h0[m])
+            product(size, 0)
+
+        @pl.when(jnp.logical_not(diagonal))
+        def _():
+            for m in range(n_mb):
+                start(h1[m])
+            finish(own)
+            finish(sib_w)
+
+        wait_h(0)
+
+        @pl.when(diagonal)
+        def _():
+            start(h1[0])
+
+        @pl.when(jnp.logical_not(diagonal))
+        def _():
+            start(h0[0])
+            finish(h0[0])
+            product(size, 0, None, (0,))
+
+        w2_x_end(0).wait_recv()
+        w2_fwd_end(0).start()
+        start(x_w[0])
+        w2_fwd_end(0).wait_recv()
+        start(f_w[0])
+        finish(h1[0])
+        finish(x_w[0])
+        finish(f_w[0])
+        product(size, 1, None, (0,), end_parts[0])
+
+        @pl.when(jnp.logical_not(diagonal))
+        def _():
+            finish(h1[1])
+            product(size, 1, None, (1,), end_parts[0])
+
+        w2_x_end(1).wait_recv()
+        w2_fwd_end(1).start()
+        start(x_w[1])
+        wait_h(1)
+
+        @pl.when(diagonal)
+        def _():
+            start(h1[1])
+            finish(h1[1])
+            product(size, 1, None, (1,), end_parts[0])
+
+        @pl.when(jnp.logical_not(diagonal))
+        def _():
+            start(h0[1])
+            finish(h0[1])
+            product(size, 0, None, (1,))
+
+        w2_fwd_end(1).wait_recv()
+        start(f_w[1])
+        finish(x_w[1])
+        finish(f_w[1])
+        product(size, 1, drain_tile, None, end_parts[1])
+
+    end_chunk()
     steps = n_mb * tok // TM
     for p, buf in enumerate((ln_a, ln_b)):
         out_copy(steps - 2 + p, buf, osem.at[p]).wait()
@@ -433,13 +545,19 @@
 
     lax.fori_loop(0, n1, sent1, 0)
     lax.fori_loop(0, full, sent2, 0)
-    for p in range(full, full + len(TAIL)):
+    for p in range(full, p_end):
         sent2(p, 0)
+    for part in range(2):
+        w2_x_end(part).wait_send()
+        w2_fwd_end(part).wait_send()
+    w2_sib(p_end).wait_send()
     lax.fori_loop(0, EARLY, sent_early, 0)
     lax.fori_loop(EARLY, n1 - 2, sent_pair, 0)
-    for u in range(len(LAST)):
-        for k in range(2):
+    for k in range(2):
+        for u in range(len(LAST) - 1):
             h_last(k, u).wait_send()
+        for m in range(n_mb):
+            h_end(k, m).wait_send()
 
 
 def solution(mesh):
@@ -450,8 +568,8 @@
         d4, hid = w1.shape
         r4 = w2.shape[0]
         n1, n2 = hid // TN, r4 // TN
-        n2p = n2 - TAIL[0][0] + len(TAIL)
-        nh = (n_mb - 1) * EARLY + n1 - 2 + 2 * len(LAST)
+        n2p = n2 - TAIL[0][0] + len(TAIL) + 1
+        nh = (n_mb - 1) * EARLY + n1 - 2 + 2 * len(LAST) + 2 * n_mb
         bf16, f32 = jnp.bfloat16, jnp.float32
         dma = pltpu.SemaphoreType.DMA
         any_spec = pl.BlockSpec(memory_space=pl.ANY)

time: 1160 us -> 1160 us (level)
  no operation moved by 1% of the time
where the time goes in v5:
time: 1160 us
  Pallas kernels  1150 us (99%)
    pallas_call x1, Pallas kernels, per_device(): pl.pallas_call(functools.partial(kernel, (n_mb, tok, dh, d4, hid, r4)), o...  1150 us

profile of v5, /device:TPU:2, one launch (start us, length us, event | category | flops | bytes accessed | tf_op | source)
XLA Modules:
  0.0 1159.6 jit_solution(2406015329979040001)
XLA Ops:
  0.0 1150.8 %shard_map.46 = (bf16[2,1024,2560]{2,1,0:T(8,128)(2,1)}, bf16[2,1024,2560]{2,1,0:T(8,128)(2,1)}, f32[20,128]{1,0:T(8,128)}, bf16[4,20,1280,512]{3,2,1,0:T(8,128)...) custom-call(bf16[2,1024,2560]{2,1,0:T(8,128)(2,1)} %x.1, f32[20,128]{1,0:T(8,128)} %bitcast.1, ...), custom_call_target="tpu_custom_call" | custom-call | tf_op jit(solution)/shard_map/pallas_call | solution.py:584
  1150.8 8.7 copy.6

commit v6 on v4

--- a/solution.py
+++ b/solution.py
@@ -11,7 +11,8 @@
 LN_EPS = 1e-5
 MESH = pl.DeviceIdType.MESH
 TN = 512
-WINDOW = 8
+TW = 2 * TN
+WINDOW = 4
 EARLY = 8
 TM = 256
 SUB = 128
@@ -28,6 +29,7 @@
     d_model = 2 * dh
     n1 = hid // TN
     n2 = r4 // TN
+    nq = hid // TW
     n_sub = TN // SUB
     last_at = [sum(LAST[:u]) for u in range(len(LAST))]
     full = n2 - TAIL[0][0]
@@ -58,14 +60,21 @@
     def g_move():
         return remote(g, gr, gs.at[0], gs.at[1], to_col)
 
-    def w1_x(s):
-        return remote(w1.at[:, cols(s)], w1_all.at[row, s], xs1.at[s], xr1.at[s], to_x)
-
-    def w1_sib(s):
-        return remote(w1.at[:, cols(s)], w1_all.at[row, s], ss1.at[s], sr1.at[s], to_sib)
-
-    def w1_fwd(s):
-        return remote(w1_all.at[xn, s], w1_all.at[xn, s], fs1.at[s], fr1.at[s], to_sib)
+    def cols_in(q):
+        return pl.ds(pl.multiple_of(lax.rem(q, 2) * r4 + (q // 2) * TW, TW), TW)
+
+    def step_of(t):
+        q = t // 2
+        return 2 * (2 * (q // 2) + lax.rem(t, 2)) + lax.rem(q, 2)
+
+    def w1_x(q):
+        return remote(w1.at[:, cols_in(q)], w1_all.at[row, q], xs1.at[q], xr1.at[q], to_x)
+
+    def w1_sib(q):
+        return remote(w1.at[:, cols_in(q)], w1_all.at[row, q], ss1.at[q], sr1.at[q], to_sib)
+
+    def w1_fwd(q):
+        return remote(w1_all.at[xn, q], w1_all.at[xn, q], fs1.at[q], fr1.at[q], to_sib)
 
     def w2_x(c):
         return remote(w2.at[rows2(c)], w2_all.at[row, rows2(c)], xs2.at[c], xr2.at[c], to_x)
@@ -106,16 +115,17 @@
 
     lax.fori_loop(0, WINDOW, first_pieces, 0)
 
-    def issue_after(s):
-        @pl.when(s + WINDOW < n1)
-        def _():
-            w1_x(s + WINDOW).start()
-            w1_sib(s + WINDOW).start()
-
-        @pl.when(s + WINDOW >= n1)
-        def _():
-            w2_x(s + WINDOW - n1).start()
-            w2_sib(s + WINDOW - n1).start()
+    def issue_after(q):
+        @pl.when(q + WINDOW < nq)
+        def _():
+            w1_x(q + WINDOW).start()
+            w1_sib(q + WINDOW).start()
+
+        @pl.when(q + WINDOW >= nq)
+        def _():
+            for i in range(2):
+                w2_x(2 * (q + WINDOW - nq) + i).start()
+                w2_sib(2 * (q + WINDOW - nq) + i).start()
 
     def layer_norm(m):
         x_move(m).wait_recv()
@@ -156,16 +166,17 @@
         w1_sib(s).wait_recv()
         w1_fwd(s).wait_recv()
 
-    def wt_copies(s):
-        base = lax.rem(s, 2) * (4 * d4)
-        sem0 = 4 * lax.rem(s, 2)
+    def wt_copies(t):
+        base = lax.rem(t, 2) * (4 * d4)
+        sem0 = 4 * lax.rem(t, 2)
+        half = pl.ds(pl.multiple_of(lax.rem(t, 2) * TN, TN), TN)
 
         def rows(b):
             return wt.at[pl.ds(pl.multiple_of(base + b * d4, d4), d4)]
 
-        copies = [pltpu.make_async_copy(w1.at[:, cols(s)], rows(row), lsem.at[sem0])]
+        copies = [pltpu.make_async_copy(w1.at[:, cols(step_of(t))], rows(row), lsem.at[sem0])]
         for j, b in enumerate((sib, xn, xs_row)):
-            copies.append(pltpu.make_async_copy(w1_all.at[b, s], rows(b), lsem.at[sem0 + j + 1]))
+            copies.append(pltpu.make_async_copy(w1_all.at[b, t // 2, :, half], rows(b), lsem.at[sem0 + j + 1]))
         return copies
 
     def load_wt(s):
@@ -176,12 +187,13 @@
         for cp in wt_copies(s):
             cp.wait()
 
-    def first_product(m, s):
-        base = pl.multiple_of(lax.rem(s, 2) * (4 * d4), 4 * d4)
-
-        def tile(t, carry):
-            rs = pl.ds(pl.multiple_of(t * TM, TM), TM)
-            zr = pl.ds(pl.multiple_of(m * tok + t * TM, TM), TM)
+    def first_product(m, t):
+        s = step_of(t)
+        base = pl.multiple_of(lax.rem(t, 2) * (4 * d4), 4 * d4)
+
+        def tile(i, carry):
+            rs = pl.ds(pl.multiple_of(i * TM, TM), TM)
+            zr = pl.ds(pl.multiple_of(m * tok + i * TM, TM), TM)
             u = jnp.dot(z[zr, :], wt[pl.ds(base, 4 * d4), :], preferred_element_type=jnp.float32)
             h = 0.5 * u * (1.0 + jnp.tanh(GELU_C * (u + 0.044715 * (u * u * u))))
             hout[rs, :] = h.astype(jnp.bfloat16)
@@ -203,42 +215,44 @@
             gv[i:i + 1, j * 128:(j + 1) * 128] = g_rows[i, j:j + 1, :]
     layer_norm(0)
 
-    def early_a(s, carry):
-        take_piece(s)
-        load_wt(s)
-        wait_wt(s)
-        first_product(0, s)
-        h_early(0, s).start()
-        return carry
-
-    def early_b(s, carry):
-        wait_wt(s)
-
-        @pl.when(s + 1 < EARLY)
-        def _():
-            load_wt(s + 1)
-
-        first_product(1, s)
-        h_early(1, s).start()
-        return carry
-
-    def both(s):
-        take_piece(s)
-        load_wt(s)
-        wait_wt(s)
+    def take_at(t):
+        @pl.when(lax.rem(t, 2) == 0)
+        def _():
+            take_piece(t // 2)
+
+    def early_a(t, carry):
+        take_at(t)
+        load_wt(t)
+        wait_wt(t)
+        first_product(0, t)
+        h_early(0, step_of(t)).start()
+        return carry
+
+    def early_b(t, carry):
+        wait_wt(t)
+
+        @pl.when(t + 1 < EARLY)
+        def _():
+            load_wt(t + 1)
+
+        first_product(1, t)
+        h_early(1, step_of(t)).start()
+        return carry
+
+    def rest(t, carry):
+        take_at(t)
+        load_wt(t)
+        wait_wt(t)
 
         def each(m, carry):
-            first_product(m, s)
+            first_product(m, t)
             return carry
 
         lax.fori_loop(0, n_mb, each, 0)
 
-    def rest(s, carry):
-        both(s)
-
-        @pl.when(s < n1 - 2)
-        def _():
-            h_pair(s).start()
+        @pl.when(step_of(t) < n1 - 2)
+        def _():
+            h_pair(step_of(t)).start()
 
         return carry
 
@@ -431,7 +445,7 @@
         h_pair(s).wait_send()
         return carry
 
-    lax.fori_loop(0, n1, sent1, 0)
+    lax.fori_loop(0, nq, sent1, 0)
     lax.fori_loop(0, full, sent2, 0)
     for p in range(full, full + len(TAIL)):
         sent2(p, 0)
@@ -459,7 +473,7 @@
             jax.ShapeDtypeStruct((n_mb, tok, dh), bf16),
             jax.ShapeDtypeStruct((n_mb, tok, dh), bf16),
             jax.ShapeDtypeStruct((dh // 128, 128), f32),
-            jax.ShapeDtypeStruct((4, n1, d4, TN), bf16),
+            jax.ShapeDtypeStruct((4, hid // TW, d4, TW), bf16),
             jax.ShapeDtypeStruct((4, r4, dh), bf16),
             jax.ShapeDtypeStruct((2, n1, n_mb, TN // SUB, tok, SUB), bf16),
         )
@@ -478,7 +492,7 @@
                 pltpu.VMEM((2, dh), f32),
                 pltpu.VMEM((n_mb * tok, dh), f32),
                 dma((n_mb,)), dma((n_mb,)), dma((2,)),
-                dma((n1,)), dma((n1,)), dma((n1,)), dma((n1,)), dma((n1,)), dma((n1,)),
+                *[dma((hid // TW,))] * 6,
                 dma((n2p,)), dma((n2p,)), dma((n2p,)), dma((n2p,)), dma((n2p,)), dma((n2p,)),
                 dma((nh,)), dma((nh,)),
                 dma((8,)), dma((8 * (TN // SUB),)), dma((2,)), dma((4 * (dh // TN),)),

time: 1160 us -> 1160 us (level)
  no operation moved by 1% of the time
where the time goes in v6:
time: 1160 us; the launch traced here: 1150 us
  Pallas kernels  1150 us (99%)
    pallas_call x1, Pallas kernels, per_device(): pl.pallas_call(functools.partial(kernel, (n_mb, tok, dh, d4, hid, r4)), o...  1150 us

profile of v6, /device:TPU:2, one launch (start us, length us, event | category | flops | bytes accessed | tf_op | source)
XLA Modules:
  0.0 1154.1 jit_solution(8071012756008789794)
XLA Ops:
  0.0 1145.4 %shard_map.46 = (bf16[2,1024,2560]{2,1,0:T(8,128)(2,1)}, bf16[2,1024,2560]{2,1,0:T(8,128)(2,1)}, f32[20,128]{1,0:T(8,128)}, bf16[4,10,1280,1024]{3,2,1,0:T(8,128...) custom-call(bf16[2,1024,2560]{2,1,0:T(8,128)(2,1)} %x.1, f32[20,128]{1,0:T(8,128)} %bitcast.1, ...), custom_call_target="tpu_custom_call" | custom-call | tf_op jit(solution)/shard_map/pallas_call | solution.py:480
  1145.4 8.7 copy.6
